TPU v7x, 256 devices: a whole 4x4x8 slice. The times are simulated.
256 devices in a mesh: ia: 16 (over y, x_hi, core), ja: 8 (over z), af: 2 (over x_lo).
Axes of the slice: x: 4 (x_hi: 2, x_lo: 2; x = x_hi * 2 + x_lo), y: 4, z: 8, core: 2. Of those that a mesh axis runs over, the one named last changes fastest.
Arguments:
- alleles: int32 [2048, 1024], P(('ia', 'ja'), 'af'), may hold values from -2147483648 to 2147483646
- section: int32 [1], replicated, may hold values from 0 to 255
Outputs:
- metric: float32 [8, 2048, 2048], P('af', 'ia', 'ja')
Inputs may be any that keep to these rules, and one draw needn't show every extreme that they name: `section`: the slab of third vectors lies inside the vector range.
All inputs are finite; a program needn't handle non-finite values.
Results may differ from a plain program's by a relative error of at most 0.0003.
Values sent between devices are 32-bit elements; how exact they have to be, the bound alone decides.
No kernel may reach another device: no remote copies, remote signals or barrier semaphores. Data moves between devices by JAX's collectives and lax.ppermute only.
A program may use at most 64 MiB of HBM per device.

v0:
```python
import jax
import jax.numpy as jnp
from jax import lax
from jax.experimental import pallas as pl
from jax.experimental.pallas import tpu as pltpu
from jax.sharding import Mesh
from jax.sharding import PartitionSpec as P


KS = 8
ROWS = 16
SIDE = ("y", "xh")
F8 = jnp.float8_e4m3fn
PLACES = {4: (0, 0), 3: (1, 0), 5: (3, 0), 2: (2, 0), 6: (0, 1), 1: (1, 1), 7: (3, 1), 0: (2, 1)}
Y_STEPS = (0, 1, 3, 2)


def broadcast_all(array, axis):
    size = lax.axis_size(axis)
    return lax.all_to_all(
        jnp.broadcast_to(array[None], (size, *array.shape)), axis, 0, 0, tiled=True
    )


def to_planes(array):
    pairs = []
    for y in range(4):
        for xh in range(2):
            for c in range(2):
                for z in range(8):
                    plane = 2 * y + xh
                    dy, dx = PLACES[(z - plane) % 8]
                    there = (((y + dy) % 4) * 2 + (xh + dx) % 2) * 2 + c
                    pairs.append((((y * 2 + xh) * 2 + c) * 8 + z, there * 8 + plane))
    return lax.ppermute(array, ("y", "xh", "c", "z"), pairs)


def swap(array, axis, bit=1):
    return lax.ppermute(array, axis, [(n, n ^ bit) for n in range(lax.axis_size(axis))])


def spread(array, axis, bit, root):
    other = swap(array, axis, bit)
    return jnp.where((lax.axis_index(axis) & bit) == (root & bit), array, other)


def bits(words, bit):
    mask = jnp.int8((1 << bit) - (1 << 8 if bit == 7 else 0))
    return jnp.where((words & mask) != 0, jnp.full(words.shape, 1, F8), jnp.full(words.shape, 0, F8))


def pieces(words):
    return [(lax.shift_right_logical(words, s) if s else words).astype(jnp.int8) for s in range(0, 32, 8)]


def popcounts(words):
    return lax.population_count(words).astype(jnp.float32)


def place_j(mine, theirs, jbuf):
    core, plane, y, xh = (lax.axis_index(a) for a in ("c", "z", "y", "xh"))
    for slot in range(8):
        y_from = y - Y_STEPS[slot // 2]
        dy = (y_from - plane // 2) & 3
        dx = (xh + slot + plane) & 1
        dz = jnp.int32(0)
        for step, (at_y, at_x) in PLACES.items():
            dz = jnp.where((dy == at_y) & (dx == at_x), step, dz)
        row = ((plane + dz) & 7) * ROWS
        own = pl.multiple_of(core * 128 + row, ROWS)
        other = pl.multiple_of((1 - core) * 128 + row, ROWS)
        jbuf[pl.ds(own, ROWS), :] = mine[slot * ROWS : (slot + 1) * ROWS, :]
        jbuf[pl.ds(other, ROWS), :] = theirs[slot * ROWS : (slot + 1) * ROWS, :]


def counts_into(acc, base, i_ref, j_ref, thirds):
    i_parts, j_parts, k_parts = pieces(i_ref[...]), pieces(j_ref[...]), pieces(thirds)
    for i_part, j_part, k_part in zip(i_parts, j_parts, k_parts):
        pairs = jnp.concatenate([i_part & k_part[t : t + 1] for t in range(4)], axis=0)
        part = lax.dot_general(
            jnp.concatenate([bits(pairs, b) for b in range(8)], axis=1),
            jnp.concatenate([bits(j_part, b) for b in range(8)], axis=1),
            (((1,), (1,)), ((), ())),
            preferred_element_type=jnp.float32,
        )
        acc[...] = part if base is None else base[...] + part
        base = acc


def ones_of(i_ref, j_ref):
    ones_i = jnp.sum(popcounts(i_ref[...]), axis=1, keepdims=True)
    j_counts = popcounts(j_ref[...]).astype(jnp.bfloat16)
    ones_j = lax.dot_general(
        jnp.ones((8, j_counts.shape[1]), jnp.bfloat16),
        j_counts,
        (((1,), (1,)), ((), ())),
        preferred_element_type=jnp.float32,
    )[0:1]
    return ones_i + ones_j


def own_half(iw, mine, theirs, thirds, acc, ones, jbuf):
    place_j(mine, theirs, jbuf)
    counts_into(acc, None, iw, jbuf, thirds[0:4])
    ones[...] = ones_of(iw, jbuf)


def other_half(iw, mine, theirs, thirds, base, ones, out, jbuf, acc):
    place_j(mine, theirs, jbuf)
    counts_into(acc, base, iw, jbuf, thirds[4:8])
    ones_k = jnp.sum(popcounts(thirds[0:4]) + popcounts(thirds[4:8]), axis=1, keepdims=True)
    ones_ij = ones[...] + ones_of(iw, jbuf) + 1.0
    for t in range(4):
        out[t] = 3.0 * acc[t * 128 : (t + 1) * 128, :] / (ones_ij + ones_k[t : t + 1])


def on_core(kernel, operands, outs, scratch):
    operands = [pltpu.with_memory_space_constraint(a, pltpu.VMEM) for a in operands]
    return pl.pallas_call(
        kernel,
        out_shape=outs,
        in_specs=[VM] * len(operands),
        out_specs=jax.tree.map(lambda _: VM, outs),
        scratch_shapes=[pltpu.VMEM(*s) for s in scratch],
        cost_estimate=COST,
    )(*operands)


VM = pl.BlockSpec(memory_space=pltpu.VMEM)
COST = pl.CostEstimate(flops=2 * 512 * 256 * 16384, bytes_accessed=2**21, transcendentals=0)


def turn(array, step):
    return lax.ppermute(array, "y", [(n, (n + step) % 4) for n in range(4)])


def per_device(alleles, section):
    words = alleles.shape[1]
    half = lax.axis_index("xl")
    row = section[0] * KS
    ia_s = row // 128
    moved = to_planes(alleles)
    iwords = broadcast_all(alleles, "z").reshape(128, words)
    pair = jnp.concatenate([moved, swap(moved, "xh")], axis=0)
    slab = lax.dynamic_slice_in_dim(iwords, lax.rem(row, 128), KS, 0).reshape(1, 2, 4, words)
    slab = jnp.broadcast_to(slab, (8, 2, 4, words)).reshape(16, 4, words)
    came = lax.all_to_all(slab, (*SIDE, "xl"), 0, 0, tiled=True).reshape(8, 2, 4, words)
    came = lax.dynamic_index_in_dim(came, ia_s // 2, 0, keepdims=False)
    k_own = lax.dynamic_index_in_dim(came, half, 0, keepdims=False)
    k_other = lax.dynamic_index_in_dim(came, 1 - half, 0, keepdims=False)
    thirds = jnp.concatenate([k_own, k_other], axis=0)
    iwords_x = swap(iwords, "xl")
    turns = [turn(pair, d) for d in Y_STEPS[1:]]
    mine = jnp.concatenate([pair, *turns], axis=0)
    thirds = spread(thirds, "c", 1, lax.rem(ia_s, 2))
    mine_x = swap(mine, "xl")
    theirs = swap(mine, "c")
    theirs_x = swap(mine_x, "c")
    j_words = ((256, words), jnp.int32)
    counts, ones = on_core(
        own_half,
        [iwords, mine, theirs, thirds],
        (pltpu.VMEM((512, 256), jnp.float32), pltpu.VMEM((128, 256), jnp.float32)),
        [j_words],
    )
    return on_core(
        other_half,
        [iwords_x, mine_x, theirs_x, thirds, counts, ones],
        jax.ShapeDtypeStruct((4, 128, 256), jnp.float32),
        [j_words, ((512, 256), jnp.float32)],
    )


def solution(mesh):
    torus = Mesh(
        mesh.devices.reshape(4, 2, 2, mesh.shape["ja"], mesh.shape["af"]),
        ("y", "xh", "c", "z", "xl"),
    )
    in_specs = (P(("y", "xh", "c", "z"), "xl"), P())
    out_specs = P("xl", ("y", "xh", "c"), "z")


    return jax.shard_map(
        per_device, mesh=torus, in_specs=in_specs, out_specs=out_specs, check_vma=False
    )
```

profile of v0, /device:TPU:32, one launch (start us, length us, event | category | flops | bytes accessed | tf_op | source)
XLA Modules:
  0.0 54.7 jit_solution(12908680383348467477)
XLA Ops:
  0.0 3.6 %collective-permute-start.1 = (s32[16,512]{1,0:T(8,128)}, s32[16,512]{1,0:T(8,128)S(1)}, u32[]{:S(2)}, u32[]{:S(2)}) collective-permute-start(s32[16,512]{1,0:T(8,128)} %param.2), channel_id=1, source_target_pairs={{0,160},{2,96},{4,128},{6,64},{8,0},{10,192},{12,32},{14,224},{16,... | collective-permute-start | bytes 98312 | tf_op jit(solution)/shard_map/ppermute | solution.py:35
  3.6 1.5 %broadcast_in_dim.6 = s32[8,16,512]{2,1,0:T(8,128)} broadcast(s32[16,512]{1,0:T(8,128)} %param.2), dimensions={1,2} | broadcast | bytes 294912 | tf_op jit(solution)/shard_map/broadcast_in_dim | solution.py:21
  5.1 5.9 %all-to-all-start = ((s32[8,16,512]{2,1,0:T(8,128)}), s32[8,16,512]{2,1,0:T(8,128)S(1)}, u32[]{:S(2)}, u32[]{:S(2)}) async-start(s32[8,16,512]{2,1,0:T(8,128)} %broadcast_in_dim.6), calls=%async_computation | async-start | bytes 524288 | tf_op jit(solution)/shard_map/all_to_all | solution.py:20
  11.0 0.0 collective-permute-done.1
  11.1 2.8 %collective-permute-start.2 = (s32[16,512]{1,0:T(8,128)S(1)}, s32[16,512]{1,0:T(8,128)S(1)}, u32[]{:S(2)}, u32[]{:S(2)}) collective-permute-start(s32[16,512]{1,0:T(8,128)S(1)} %collective-permute-done.1), channel_id=1, source_target_pairs={{0,32},{32,0},{1,33},{33,1},{2,34},{34,2},{3,35},{35,3},{4,36},{36... | collective-permute-start | bytes 98312 | tf_op jit(solution)/shard_map/ppermute | solution.py:39
  13.9 2.6 %collective-permute-done.2 = s32[16,512]{1,0:T(8,128)S(1)} collective-permute-done((s32[16,512]{1,0:T(8,128)S(1)}, s32[16,512]{1,0:T(8,128)S(1)}, u32[]{:S(2)}, u32[]{:S(2)}) %collective-permute-start.2) | collective-permute-done | bytes 32800 | tf_op jit(solution)/shard_map/ppermute | solution.py:39
  16.5 2.0 %collective-permute-start.3 = (s32[32,512]{1,0:T(8,128)S(1)}, s32[32,512]{1,0:T(8,128)S(1)}, u32[]{:S(2)}, u32[]{:S(2)}) collective-permute-start(s32[32,512]{1,0:T(8,128)S(1)} %get-tuple-element.11), channel_id=1, source_target_pairs={{0,64},{64,128},{128,192},{192,0},{1,65},{65,129},{129,193},{193,1... | collective-permute-start | bytes 196616 | tf_op jit(solution)/shard_map/ppermute | solution.py:134
  19.1 5.5 %collective-permute-start.5 = (s32[32,512]{1,0:T(8,128)S(1)}, s32[32,512]{1,0:T(8,128)S(1)}, u32[]{:S(2)}, u32[]{:S(2)}) collective-permute-start(s32[32,512]{1,0:T(8,128)S(1)} %get-tuple-element.11), channel_id=1, source_target_pairs={{0,128},{64,192},{128,0},{192,64},{1,129},{65,193},{129,1},{193,65... | collective-permute-start | bytes 196616 | tf_op jit(solution)/shard_map/ppermute | solution.py:134
  24.7 1.2 %collective-permute-start.4 = (s32[32,512]{1,0:T(8,128)S(1)}, s32[32,512]{1,0:T(8,128)S(1)}, u32[]{:S(2)}, u32[]{:S(2)}) collective-permute-start(s32[32,512]{1,0:T(8,128)S(1)} %get-tuple-element.11), channel_id=1, source_target_pairs={{0,192},{64,0},{128,64},{192,128},{1,193},{65,1},{129,65},{193,129... | collective-permute-start | bytes 196616 | tf_op jit(solution)/shard_map/ppermute | solution.py:134
  25.8 0.0 collective-permute-done.3
  25.9 3.1 %collective-permute-done.4 = s32[32,512]{1,0:T(8,128)S(1)} collective-permute-done((s32[32,512]{1,0:T(8,128)S(1)}, s32[32,512]{1,0:T(8,128)S(1)}, u32[]{:S(2)}, u32[]{:S(2)}) %collective-permute-start.4) | collective-permute-done | bytes 65568 | tf_op jit(solution)/shard_map/ppermute | solution.py:134
  29.0 0.0 all-to-all-done
  29.0 0.7 %broadcast_in_dim.15 = s32[8,2,4,512]{3,2,1,0:T(4,128)} broadcast(s32[2,4,512]{2,1,0:T(4,128)S(1)} %broadcast_in_dim.14), dimensions={1,2,3} | broadcast | bytes 147456 | tf_op jit(solution)/shard_map/broadcast_in_dim | solution.py:146
  29.7 4.8 %all-to-all-start.1 = ((s32[16,4,512]{2,1,0:T(4,128)}), s32[16,4,512]{2,1,0:T(4,128)S(1)}, u32[]{:S(2)}, u32[]{:S(2)}) async-start(s32[16,4,512]{2,1,0:T(4,128)} %bitcast.2), calls=%async_computation.1 | async-start | bytes 262144 | tf_op jit(solution)/shard_map/all_to_all | solution.py:147
  34.5 0.0 collective-permute-done.5
  34.5 2.0 %collective-permute-start.6 = (s32[128,512]{1,0:T(8,128)S(1)}, s32[128,512]{1,0:T(8,128)S(1)}, u32[]{:S(2)}, u32[]{:S(2)}) collective-permute-start(s32[128,512]{1,0:T(8,128)S(1)} %constant_dynamic-update-slice_fusion.2.mine), channel_id=1, source_target_pairs={{0,1},{1,0},{2,3},{3,2},{4,5},{5,4},{6,7},{7,6},{8,9},{9,8},{10,11... | collective-permute-start | bytes 786440 | tf_op jit(solution)/shard_map/ppermute | solution.py:39
  36.5 0.0 collective-permute-start.9
  36.5 6.0 %all-to-all-done.1 = s32[16,4,512]{2,1,0:T(4,128)S(1)} async-done(((s32[16,4,512]{2,1,0:T(4,128)}), s32[16,4,512]{2,1,0:T(4,128)S(1)}, u32[]{:S(2)}, u32[]{:S(2)}) %all-to-all-start.1) | async-done | bytes 131104 | tf_op jit(solution)/shard_map/all_to_all | solution.py:147
  42.5 0.1 collective-permute-start.8
  42.6 0.0 collective-permute-done.6.mine
  42.6 0.5 collective-permute-start.7
  43.1 0.6 %collective-permute-start = (s32[128,512]{1,0:T(8,128)S(1)}, s32[128,512]{1,0:T(8,128)S(1)}, u32[]{:S(2)}, u32[]{:S(2)}) collective-permute-start(s32[128,512]{1,0:T(8,128)S(1)} %bitcast.9), channel_id=1, source_target_pairs={{0,1},{1,0},{2,3},{3,2},{4,5},{5,4},{6,7},{7,6},{8,9},{9,8},{10,11... | collective-permute-start | bytes 786440 | tf_op jit(solution)/shard_map/ppermute | solution.py:39
  43.6 0.1 collective-permute-done.8
  43.7 0.0 collective-permute-done.9.theirs
  43.8 2.5 %shard_map.28 = (f32[512,256]{1,0:T(8,128)S(1)}, f32[128,256]{1,0:T(8,128)S(1)}) custom-call(s32[128,512]{1,0:T(8,128)S(1)} %bitcast.10, s32[128,512]{1,0:T(8,128)S(1)} %constant_dynamic-update-slice_fusion.2.mine, s32[128,512]{1,0:T(8,128)S(1)} %collective-permute-done.9.theirs, s32[8,512]{1,0:T(8,128)S(1)} %broadcast_select_fusion.thirds), custom_call_target="tpu_custom_call" | custom-call | flops 4294967296 | bytes 2097152 | tf_op jit(solution)/shard_map/pallas_call | solution.py:119
  46.3 0.0 collective-permute-done.7.theirs
  46.3 5.1 %collective-permute-done.iw = s32[128,512]{1,0:T(8,128)S(1)} collective-permute-done((s32[128,512]{1,0:T(8,128)S(1)}, s32[128,512]{1,0:T(8,128)S(1)}, u32[]{:S(2)}, u32[]{:S(2)}) %collective-permute-start) | collective-permute-done | bytes 262176 | tf_op jit(solution)/shard_map/ppermute | solution.py:39
  51.4 3.3 %shard_map.29 = f32[4,128,256]{2,1,0:T(8,128)} custom-call(s32[128,512]{1,0:T(8,128)S(1)} %collective-permute-done.iw, s32[128,512]{1,0:T(8,128)S(1)} %collective-permute-done.6.mine, s32[128,512]{1,0:T(8,128)S(1)} %collective-permute-done.7.theirs, s32[8,512]{1,0:T(8,128)S(1)} %broadcast_select_fusion.thirds, f32[512,256]{1,0:T(8,128)S(1)} %get-tuple-element.7.base, ...), custom_call_target="tpu_custom_call" | custom-call | flops 4294967296 | bytes 2097152 | tf_op jit(solution)/shard_map/pallas_call | solution.py:119
  (10 shorter events, 0.1 us)
Async XLA Ops:
  0.0 11.0 %collective-permute-start.1 = (s32[16,512]{1,0:T(8,128)}, s32[16,512]{1,0:T(8,128)S(1)}, u32[]{:S(2)}, u32[]{:S(2)}) collective-permute-start(s32[16,512]{1,0:T(8,128)} %param.2), channel_id=1, source_target_pairs={{0,160},{2,96},{4,128},{6,64},{8,0},{10,192},{12,32},{14,224},{16,... | collective-permute-start | bytes 98312 | tf_op jit(solution)/shard_map/ppermute | solution.py:35
  5.1 23.9 %all-to-all-start = ((s32[8,16,512]{2,1,0:T(8,128)}), s32[8,16,512]{2,1,0:T(8,128)S(1)}, u32[]{:S(2)}, u32[]{:S(2)}) async-start(s32[8,16,512]{2,1,0:T(8,128)} %broadcast_in_dim.6), calls=%async_computation | async-start | bytes 524288 | tf_op jit(solution)/shard_map/all_to_all | solution.py:20
  11.1 5.4 %collective-permute-start.2 = (s32[16,512]{1,0:T(8,128)S(1)}, s32[16,512]{1,0:T(8,128)S(1)}, u32[]{:S(2)}, u32[]{:S(2)}) collective-permute-start(s32[16,512]{1,0:T(8,128)S(1)} %collective-permute-done.1), channel_id=1, source_target_pairs={{0,32},{32,0},{1,33},{33,1},{2,34},{34,2},{3,35},{35,3},{4,36},{36... | collective-permute-start | bytes 98312 | tf_op jit(solution)/shard_map/ppermute | solution.py:39
  16.5 9.4 %collective-permute-start.3 = (s32[32,512]{1,0:T(8,128)S(1)}, s32[32,512]{1,0:T(8,128)S(1)}, u32[]{:S(2)}, u32[]{:S(2)}) collective-permute-start(s32[32,512]{1,0:T(8,128)S(1)} %get-tuple-element.11), channel_id=1, source_target_pairs={{0,64},{64,128},{128,192},{192,0},{1,65},{65,129},{129,193},{193,1... | collective-permute-start | bytes 196616 | tf_op jit(solution)/shard_map/ppermute | solution.py:134
  19.1 15.3 %collective-permute-start.5 = (s32[32,512]{1,0:T(8,128)S(1)}, s32[32,512]{1,0:T(8,128)S(1)}, u32[]{:S(2)}, u32[]{:S(2)}) collective-permute-start(s32[32,512]{1,0:T(8,128)S(1)} %get-tuple-element.11), channel_id=1, source_target_pairs={{0,128},{64,192},{128,0},{192,64},{1,129},{65,193},{129,1},{193,65... | collective-permute-start | bytes 196616 | tf_op jit(solution)/shard_map/ppermute | solution.py:134
  24.7 4.3 %collective-permute-start.4 = (s32[32,512]{1,0:T(8,128)S(1)}, s32[32,512]{1,0:T(8,128)S(1)}, u32[]{:S(2)}, u32[]{:S(2)}) collective-permute-start(s32[32,512]{1,0:T(8,128)S(1)} %get-tuple-element.11), channel_id=1, source_target_pairs={{0,192},{64,0},{128,64},{192,128},{1,193},{65,1},{129,65},{193,129... | collective-permute-start | bytes 196616 | tf_op jit(solution)/shard_map/ppermute | solution.py:134
  29.7 12.8 %all-to-all-start.1 = ((s32[16,4,512]{2,1,0:T(4,128)}), s32[16,4,512]{2,1,0:T(4,128)S(1)}, u32[]{:S(2)}, u32[]{:S(2)}) async-start(s32[16,4,512]{2,1,0:T(4,128)} %bitcast.2), calls=%async_computation.1 | async-start | bytes 262144 | tf_op jit(solution)/shard_map/all_to_all | solution.py:147
  34.5 8.1 %collective-permute-start.6 = (s32[128,512]{1,0:T(8,128)S(1)}, s32[128,512]{1,0:T(8,128)S(1)}, u32[]{:S(2)}, u32[]{:S(2)}) collective-permute-start(s32[128,512]{1,0:T(8,128)S(1)} %constant_dynamic-update-slice_fusion.2.mine), channel_id=1, source_target_pairs={{0,1},{1,0},{2,3},{3,2},{4,5},{5,4},{6,7},{7,6},{8,9},{9,8},{10,11... | collective-permute-start | bytes 786440 | tf_op jit(solution)/shard_map/ppermute | solution.py:39
  36.5 7.3 %collective-permute-start.9 = (s32[128,512]{1,0:T(8,128)S(1)}, s32[128,512]{1,0:T(8,128)S(1)}, u32[]{:S(2)}, u32[]{:S(2)}) collective-permute-start(s32[128,512]{1,0:T(8,128)S(1)} %constant_dynamic-update-slice_fusion.2.mine), channel_id=1, source_target_pairs={{0,16},{16,0},{1,17},{17,1},{2,18},{18,2},{3,19},{19,3},{4,20},{20... | collective-permute-start | bytes 786440 | tf_op jit(solution)/shard_map/ppermute | solution.py:39
  42.5 1.3 %collective-permute-start.8 = (s32[8,512]{1,0:T(8,128)S(1)}, s32[8,512]{1,0:T(8,128)S(1)}, u32[]{:S(2)}, u32[]{:S(2)}) collective-permute-start(s32[8,512]{1,0:T(8,128)S(1)} %pad_add_fusion), channel_id=1, source_target_pairs={{0,16},{16,0},{1,17},{17,1},{2,18},{18,2},{3,19},{19,3},{4,20},{20... | collective-permute-start | bytes 49160 | tf_op jit(solution)/shard_map/ppermute | solution.py:39
  42.6 3.7 %collective-permute-start.7 = (s32[128,512]{1,0:T(8,128)S(1)}, s32[128,512]{1,0:T(8,128)S(1)}, u32[]{:S(2)}, u32[]{:S(2)}) collective-permute-start(s32[128,512]{1,0:T(8,128)S(1)} %collective-permute-done.6.mine), channel_id=1, source_target_pairs={{0,16},{16,0},{1,17},{17,1},{2,18},{18,2},{3,19},{19,3},{4,20},{20... | collective-permute-start | bytes 786440 | tf_op jit(solution)/shard_map/ppermute | solution.py:39
  43.1 8.3 %collective-permute-start = (s32[128,512]{1,0:T(8,128)S(1)}, s32[128,512]{1,0:T(8,128)S(1)}, u32[]{:S(2)}, u32[]{:S(2)}) collective-permute-start(s32[128,512]{1,0:T(8,128)S(1)} %bitcast.9), channel_id=1, source_target_pairs={{0,1},{1,0},{2,3},{3,2},{4,5},{5,4},{6,7},{7,6},{8,9},{9,8},{10,11... | collective-permute-start | bytes 786440 | tf_op jit(solution)/shard_map/ppermute | solution.py:39
where the time goes:
time: 55.4 us; the launch traced here: 54.7 us
  starting transfers between devices  29 us (52%)
  waiting for transfers between devices  16.9 us (31%)
  Pallas kernels  5.81 us (10%)
  local copies, waits for them, and re-layouts  2.25 us (4%)
  between operations  0.78 us (1%)
    ppermute x3, starting transfers between devices, turn(): return lax.ppermute(array, 'y', [(n, (n + step) % 4) for n in range(4)])  8.7 us
    ppermute x6, waiting for transfers between devices, swap(): lax.ppermute(array, axis, [(n, n ^ bit) for n in range(lax.axis_size(axis...  7.84 us
    ppermute x6, starting transfers between devices, swap(): lax.ppermute(array, axis, [(n, n ^ bit) for n in range(lax.axis_size(axis...  5.96 us
    all_to_all x1, waiting for transfers between devices, per_device(): lax.all_to_all(slab, (*SIDE, 'xl'), 0, 0, tiled=True)  5.95 us
    all_to_all x1, starting transfers between devices, broadcast_all(): lax.all_to_all(jnp.broadcast_to(array[None], (size, *array.shape)), axis,...  5.95 us
    pallas_call x2, Pallas kernels, on_core(): pl.pallas_call(kernel, out_shape=outs, in_specs=[VM] * len(operands), out...  5.81 us
    all_to_all x1, starting transfers between devices, per_device(): lax.all_to_all(slab, (*SIDE, 'xl'), 0, 0, tiled=True)  4.78 us
    ppermute x1, starting transfers between devices, to_planes(): return lax.ppermute(array, ('y', 'xh', 'c', 'z'), pairs)  3.58 us
  transfers between devices with their start and end apart: 12, of which 5 were waited for; matrix products, arithmetic and copies ran while one was open for 4% of the time, Pallas kernels for 5%

commit v1 on v0

--- a/solution.py
+++ b/solution.py
@@ -39,6 +39,10 @@
     return lax.ppermute(array, axis, [(n, n ^ bit) for n in range(lax.axis_size(axis))])
 
 
+def cross(array):
+    return lax.ppermute(array, ("xh", "xl"), [(n, 3 - n) for n in range(4)])
+
+
 def spread(array, axis, bit, root):
     other = swap(array, axis, bit)
     return jnp.where((lax.axis_index(axis) & bit) == (root & bit), array, other)
@@ -57,7 +61,7 @@
     return lax.population_count(words).astype(jnp.float32)
 
 
-def place_j(mine, theirs, jbuf):
+def place_j(mine, theirs, jbuf, half):
     core, plane, y, xh = (lax.axis_index(a) for a in ("c", "z", "y", "xh"))
     for slot in range(8):
         y_from = y - Y_STEPS[slot // 2]
@@ -69,8 +73,9 @@
         row = ((plane + dz) & 7) * ROWS
         own = pl.multiple_of(core * 128 + row, ROWS)
         other = pl.multiple_of((1 - core) * 128 + row, ROWS)
-        jbuf[pl.ds(own, ROWS), :] = mine[slot * ROWS : (slot + 1) * ROWS, :]
-        jbuf[pl.ds(other, ROWS), :] = theirs[slot * ROWS : (slot + 1) * ROWS, :]
+        source = slice((slot // 2 * 4 + half * 2 + slot % 2) * ROWS, (slot // 2 * 4 + half * 2 + slot % 2 + 1) * ROWS)
+        jbuf[pl.ds(own, ROWS), :] = mine[source, :]
+        jbuf[pl.ds(other, ROWS), :] = theirs[source, :]
 
 
 def counts_into(acc, base, i_ref, j_ref, thirds):
@@ -99,17 +104,13 @@
     return ones_i + ones_j
 
 
-def own_half(iw, mine, theirs, thirds, acc, ones, jbuf):
-    place_j(mine, theirs, jbuf)
+def metric(iw, iw_x, mine, theirs, thirds, out, jbuf, jbuf_x, acc):
+    place_j(mine, theirs, jbuf, 0)
+    place_j(mine, theirs, jbuf_x, 1)
     counts_into(acc, None, iw, jbuf, thirds[0:4])
-    ones[...] = ones_of(iw, jbuf)
-
-
-def other_half(iw, mine, theirs, thirds, base, ones, out, jbuf, acc):
-    place_j(mine, theirs, jbuf)
-    counts_into(acc, base, iw, jbuf, thirds[4:8])
+    counts_into(acc, acc, iw_x, jbuf_x, thirds[4:8])
     ones_k = jnp.sum(popcounts(thirds[0:4]) + popcounts(thirds[4:8]), axis=1, keepdims=True)
-    ones_ij = ones[...] + ones_of(iw, jbuf) + 1.0
+    ones_ij = ones_of(iw, jbuf) + ones_of(iw_x, jbuf_x) + 1.0
     for t in range(4):
         out[t] = 3.0 * acc[t * 128 : (t + 1) * 128, :] / (ones_ij + ones_k[t : t + 1])
 
@@ -127,7 +128,7 @@
 
 
 VM = pl.BlockSpec(memory_space=pltpu.VMEM)
-COST = pl.CostEstimate(flops=2 * 512 * 256 * 16384, bytes_accessed=2**21, transcendentals=0)
+COST = pl.CostEstimate(flops=2 * 512 * 256 * 32768, bytes_accessed=2**21, transcendentals=0)
 
 
 def turn(array, step):
@@ -141,33 +142,28 @@
     ia_s = row // 128
     moved = to_planes(alleles)
     iwords = broadcast_all(alleles, "z").reshape(128, words)
-    pair = jnp.concatenate([moved, swap(moved, "xh")], axis=0)
-    slab = lax.dynamic_slice_in_dim(iwords, lax.rem(row, 128), KS, 0).reshape(1, 2, 4, words)
-    slab = jnp.broadcast_to(slab, (8, 2, 4, words)).reshape(16, 4, words)
+    quad = jnp.concatenate(
+        [moved, swap(moved, "xh"), swap(moved, "xl"), cross(moved)],
+        axis=0,
+    )
+    slab = lax.dynamic_slice_in_dim(iwords, lax.rem(row, 128), KS, 0)
+    slab = spread(slab, "c", 1, lax.rem(ia_s, 2))
+    slab = jnp.broadcast_to(slab.reshape(1, 2, 4, words), (8, 2, 4, words)).reshape(16, 4, words)
     came = lax.all_to_all(slab, (*SIDE, "xl"), 0, 0, tiled=True).reshape(8, 2, 4, words)
     came = lax.dynamic_index_in_dim(came, ia_s // 2, 0, keepdims=False)
     k_own = lax.dynamic_index_in_dim(came, half, 0, keepdims=False)
     k_other = lax.dynamic_index_in_dim(came, 1 - half, 0, keepdims=False)
     thirds = jnp.concatenate([k_own, k_other], axis=0)
     iwords_x = swap(iwords, "xl")
-    turns = [turn(pair, d) for d in Y_STEPS[1:]]
-    mine = jnp.concatenate([pair, *turns], axis=0)
-    thirds = spread(thirds, "c", 1, lax.rem(ia_s, 2))
-    mine_x = swap(mine, "xl")
+    turns = [turn(quad, d) for d in Y_STEPS[1:]]
+    mine = jnp.concatenate([quad, *turns], axis=0)
     theirs = swap(mine, "c")
-    theirs_x = swap(mine_x, "c")
     j_words = ((256, words), jnp.int32)
-    counts, ones = on_core(
-        own_half,
-        [iwords, mine, theirs, thirds],
-        (pltpu.VMEM((512, 256), jnp.float32), pltpu.VMEM((128, 256), jnp.float32)),
-        [j_words],
-    )
     return on_core(
-        other_half,
-        [iwords_x, mine_x, theirs_x, thirds, counts, ones],
+        metric,
+        [iwords, iwords_x, mine, theirs, thirds],
         jax.ShapeDtypeStruct((4, 128, 256), jnp.float32),
-        [j_words, ((512, 256), jnp.float32)],
+        [j_words, j_words, ((512, 256), jnp.float32)],
     )
 
 
@@ -180,6 +176,4 @@
     out_specs = P("xl", ("y", "xh", "c"), "z")
 
 
-    return jax.shard_map(
-        per_device, mesh=torus, in_specs=in_specs, out_specs=out_specs, check_vma=False
-    )
+    return jax.shard_map(per_device, mesh=torus, in_specs=in_specs, out_specs=out_specs, check_vma=False)

time: 55.4 us -> 54.3 us (0.980)
  waiting for transfers between devices: 16.9 us -> 15.8 us
    ppermute x6 -> x5, waiting for transfers between devices: 7.84 us -> 4.7 us  [swap(): lax.ppermute(array, axis, [(n, n ^ bit) for n in range(lax.axis_size(axis...]
    ppermute x0 -> x1, starting transfers between devices: none -> 2.55 us  [cross(): return lax.ppermute(array, ('xh', 'xl'), [(n, 3 - n) for n in range(4)])]
    ppermute x3, starting transfers between devices: 8.7 us -> 6.95 us  [turn(): return lax.ppermute(array, 'y', [(n, (n + step) % 4) for n in range(4)])]
    ppermute x6 -> x5, starting transfers between devices: 5.96 us -> 4.26 us  [swap(): lax.ppermute(array, axis, [(n, n ^ bit) for n in range(lax.axis_size(axis...]
    ppermute x3, waiting for transfers between devices: 3.1 us -> 4.34 us  [turn(): return lax.ppermute(array, 'y', [(n, (n + step) % 4) for n in range(4)])]
    all_to_all x1, starting transfers between devices: 4.78 us -> 5.93 us  [per_device(): lax.all_to_all(slab, (*SIDE, 'xl'), 0, 0, tiled=True)]
    all_to_all x1, waiting for transfers between devices: 5.95 us -> 6.76 us  [per_device(): lax.all_to_all(slab, (*SIDE, 'xl'), 0, 0, tiled=True)]
    pallas_call x2 -> x1, Pallas kernels: 5.81 us -> 5.56 us  [on_core(): pl.pallas_call(kernel, out_shape=outs, in_specs=[VM] * len(operands), out...]
  transfers between devices with their start and end apart: 12 -> 12, of which waited for: 5 -> 5; matrix products, arithmetic and copies ran while one was open for 4% -> 4% of each run, Pallas kernels for 5% -> 0%
where the time goes in v1:
time: 54.3 us; the launch traced here: 53.7 us
  starting transfers between devices  29.2 us (54%)
  waiting for transfers between devices  15.8 us (29%)
  Pallas kernels  5.56 us (10%)
  local copies, waits for them, and re-layouts  2.27 us (4%)
  between operations  0.82 us (2%)
    ppermute x3, starting transfers between devices, turn(): return lax.ppermute(array, 'y', [(n, (n + step) % 4) for n in range(4)])  6.95 us
    all_to_all x1, waiting for transfers between devices, per_device(): lax.all_to_all(slab, (*SIDE, 'xl'), 0, 0, tiled=True)  6.76 us
    all_to_all x1, starting transfers between devices, broadcast_all(): lax.all_to_all(jnp.broadcast_to(array[None], (size, *array.shape)), axis,...  5.95 us
    all_to_all x1, starting transfers between devices, per_device(): lax.all_to_all(slab, (*SIDE, 'xl'), 0, 0, tiled=True)  5.93 us
    pallas_call x1, Pallas kernels, on_core(): pl.pallas_call(kernel, out_shape=outs, in_specs=[VM] * len(operands), out...  5.56 us
    ppermute x5, waiting for transfers between devices, swap(): lax.ppermute(array, axis, [(n, n ^ bit) for n in range(lax.axis_size(axis...  4.7 us
    ppermute x3, waiting for transfers between devices, turn(): return lax.ppermute(array, 'y', [(n, (n + step) % 4) for n in range(4)])  4.34 us
    ppermute x5, starting transfers between devices, swap(): lax.ppermute(array, axis, [(n, n ^ bit) for n in range(lax.axis_size(axis...  4.26 us
  transfers between devices with their start and end apart: 12, of which 5 were waited for; matrix products, arithmetic and copies ran while one was open for 4% of the time, Pallas kernels for 0%

profile of v1, /device:TPU:32, one launch (start us, length us, event | category | flops | bytes accessed | tf_op | source)
XLA Modules:
  0.0 53.7 jit_solution(14497517323449938598)
XLA Ops:
  0.0 3.6 %collective-permute-start.1 = (s32[16,512]{1,0:T(8,128)}, s32[16,512]{1,0:T(8,128)S(1)}, u32[]{:S(2)}, u32[]{:S(2)}) collective-permute-start(s32[16,512]{1,0:T(8,128)} %param.2), channel_id=1, source_target_pairs={{0,160},{2,96},{4,128},{6,64},{8,0},{10,192},{12,32},{14,224},{16,... | collective-permute-start | bytes 98312 | tf_op jit(solution)/shard_map/ppermute | solution.py:35
  3.6 1.5 %broadcast_in_dim.6 = s32[8,16,512]{2,1,0:T(8,128)} broadcast(s32[16,512]{1,0:T(8,128)} %param.2), dimensions={1,2} | broadcast | bytes 294912 | tf_op jit(solution)/shard_map/broadcast_in_dim | solution.py:21
  5.1 5.9 %all-to-all-start = ((s32[8,16,512]{2,1,0:T(8,128)}), s32[8,16,512]{2,1,0:T(8,128)S(1)}, u32[]{:S(2)}, u32[]{:S(2)}) async-start(s32[8,16,512]{2,1,0:T(8,128)} %broadcast_in_dim.6), calls=%async_computation | async-start | bytes 524288 | tf_op jit(solution)/shard_map/all_to_all | solution.py:20
  11.0 0.0 collective-permute-done.1
  11.1 2.6 %collective-permute-start.4 = (s32[16,512]{1,0:T(8,128)S(1)}, s32[16,512]{1,0:T(8,128)S(1)}, u32[]{:S(2)}, u32[]{:S(2)}) collective-permute-start(s32[16,512]{1,0:T(8,128)S(1)} %collective-permute-done.1), channel_id=1, source_target_pairs={{0,33},{1,32},{32,1},{33,0},{2,35},{3,34},{34,3},{35,2},{4,37},{5,... | collective-permute-start | bytes 98312 | tf_op jit(solution)/shard_map/ppermute | solution.py:43
  13.6 0.2 collective-permute-start.3
  13.8 1.9 %collective-permute-start.2 = (s32[16,512]{1,0:T(8,128)S(1)}, s32[16,512]{1,0:T(8,128)S(1)}, u32[]{:S(2)}, u32[]{:S(2)}) collective-permute-start(s32[16,512]{1,0:T(8,128)S(1)} %collective-permute-done.1), channel_id=1, source_target_pairs={{0,32},{32,0},{1,33},{33,1},{2,34},{34,2},{3,35},{35,3},{4,36},{36... | collective-permute-start | bytes 98312 | tf_op jit(solution)/shard_map/ppermute | solution.py:39
  15.8 3.5 %collective-permute-done.2 = s32[16,512]{1,0:T(8,128)S(1)} collective-permute-done((s32[16,512]{1,0:T(8,128)S(1)}, s32[16,512]{1,0:T(8,128)S(1)}, u32[]{:S(2)}, u32[]{:S(2)}) %collective-permute-start.2) | collective-permute-done | bytes 32800 | tf_op jit(solution)/shard_map/ppermute | solution.py:39
  19.3 0.0 collective-permute-done.3
  19.3 0.0 collective-permute-done.4
  19.3 2.7 %collective-permute-start.5 = (s32[64,512]{1,0:T(8,128)S(1)}, s32[64,512]{1,0:T(8,128)S(1)}, u32[]{:S(2)}, u32[]{:S(2)}) collective-permute-start(s32[64,512]{1,0:T(8,128)S(1)} %get-tuple-element.7), channel_id=1, source_target_pairs={{0,64},{64,128},{128,192},{192,0},{1,65},{65,129},{129,193},{193,1... | collective-permute-start | bytes 393224 | tf_op jit(solution)/shard_map/ppermute | solution.py:135
  22.0 2.2 %collective-permute-start.6 = (s32[64,512]{1,0:T(8,128)S(1)}, s32[64,512]{1,0:T(8,128)S(1)}, u32[]{:S(2)}, u32[]{:S(2)}) collective-permute-start(s32[64,512]{1,0:T(8,128)S(1)} %get-tuple-element.7), channel_id=1, source_target_pairs={{0,192},{64,0},{128,64},{192,128},{1,193},{65,1},{129,65},{193,129... | collective-permute-start | bytes 393224 | tf_op jit(solution)/shard_map/ppermute | solution.py:135
  24.9 2.0 %collective-permute-start.7 = (s32[64,512]{1,0:T(8,128)S(1)}, s32[64,512]{1,0:T(8,128)S(1)}, u32[]{:S(2)}, u32[]{:S(2)}) collective-permute-start(s32[64,512]{1,0:T(8,128)S(1)} %get-tuple-element.7), channel_id=1, source_target_pairs={{0,128},{64,192},{128,0},{192,64},{1,129},{65,193},{129,1},{193,65... | collective-permute-start | bytes 393224 | tf_op jit(solution)/shard_map/ppermute | solution.py:135
  26.9 1.5 %collective-permute-done.5 = s32[64,512]{1,0:T(8,128)S(1)} collective-permute-done((s32[64,512]{1,0:T(8,128)S(1)}, s32[64,512]{1,0:T(8,128)S(1)}, u32[]{:S(2)}, u32[]{:S(2)}) %collective-permute-start.5) | collective-permute-done | bytes 131104 | tf_op jit(solution)/shard_map/ppermute | solution.py:135
  28.5 0.0 collective-permute-done.6
  28.5 0.0 all-to-all-done
  28.5 0.1 collective-permute-start.9
  28.6 2.8 %collective-permute-done.7 = s32[64,512]{1,0:T(8,128)S(1)} collective-permute-done((s32[64,512]{1,0:T(8,128)S(1)}, s32[64,512]{1,0:T(8,128)S(1)}, u32[]{:S(2)}, u32[]{:S(2)}) %collective-permute-start.7) | collective-permute-done | bytes 131104 | tf_op jit(solution)/shard_map/ppermute | solution.py:135
  31.5 0.1 collective-permute-start.8
  31.6 0.0 collective-permute-done.9
  31.6 0.7 %broadcast_in_dim.15 = s32[8,2,4,512]{3,2,1,0:T(4,128)} broadcast(s32[2,4,512]{2,1,0:T(4,128)S(1)} %broadcast_in_dim.14), dimensions={1,2,3} | broadcast | bytes 147456 | tf_op jit(solution)/shard_map/broadcast_in_dim | solution.py:151
  32.3 5.9 %all-to-all-start.1 = ((s32[16,4,512]{2,1,0:T(4,128)}), s32[16,4,512]{2,1,0:T(4,128)S(1)}, u32[]{:S(2)}, u32[]{:S(2)}) async-start(s32[16,4,512]{2,1,0:T(4,128)} %bitcast.2), calls=%async_computation.1 | async-start | bytes 262144 | tf_op jit(solution)/shard_map/all_to_all | solution.py:152
  38.2 1.9 %collective-permute-start = (s32[128,512]{1,0:T(8,128)S(1)}, s32[128,512]{1,0:T(8,128)S(1)}, u32[]{:S(2)}, u32[]{:S(2)}) collective-permute-start(s32[128,512]{1,0:T(8,128)S(1)} %bitcast.10), channel_id=1, source_target_pairs={{0,1},{1,0},{2,3},{3,2},{4,5},{5,4},{6,7},{7,6},{8,9},{9,8},{10,11... | collective-permute-start | bytes 786440 | tf_op jit(solution)/shard_map/ppermute | solution.py:39
  40.2 6.8 %all-to-all-done.1 = s32[16,4,512]{2,1,0:T(4,128)S(1)} async-done(((s32[16,4,512]{2,1,0:T(4,128)}), s32[16,4,512]{2,1,0:T(4,128)S(1)}, u32[]{:S(2)}, u32[]{:S(2)}) %all-to-all-start.1) | async-done | bytes 131104 | tf_op jit(solution)/shard_map/all_to_all | solution.py:152
  46.9 0.0 collective-permute-done.8.theirs
  46.9 1.2 %collective-permute-done.iw_x = s32[128,512]{1,0:T(8,128)S(1)} collective-permute-done((s32[128,512]{1,0:T(8,128)S(1)}, s32[128,512]{1,0:T(8,128)S(1)}, u32[]{:S(2)}, u32[]{:S(2)}) %collective-permute-start) | collective-permute-done | bytes 262176 | tf_op jit(solution)/shard_map/ppermute | solution.py:39
  48.1 5.6 %shard_map.28 = f32[4,128,256]{2,1,0:T(8,128)} custom-call(s32[128,512]{1,0:T(8,128)S(1)} %bitcast.11, s32[128,512]{1,0:T(8,128)S(1)} %collective-permute-done.iw_x, s32[256,512]{1,0:T(8,128)S(1)} %constant_dynamic-update-slice_fusion.4.mine, s32[256,512]{1,0:T(8,128)S(1)} %collective-permute-done.8.theirs, s32[8,512]{1,0:T(8,128)S(1)} %pad_add_fusion.thirds), custom_call_target="tpu_custom_call" | custom-call | flops 8589934592 | bytes 2097152 | tf_op jit(solution)/shard_map/pallas_call | solution.py:120
  (12 shorter events, 0.1 us)
Async XLA Ops:
  0.0 11.0 %collective-permute-start.1 = (s32[16,512]{1,0:T(8,128)}, s32[16,512]{1,0:T(8,128)S(1)}, u32[]{:S(2)}, u32[]{:S(2)}) collective-permute-start(s32[16,512]{1,0:T(8,128)} %param.2), channel_id=1, source_target_pairs={{0,160},{2,96},{4,128},{6,64},{8,0},{10,192},{12,32},{14,224},{16,... | collective-permute-start | bytes 98312 | tf_op jit(solution)/shard_map/ppermute | solution.py:35
  5.1 23.4 %all-to-all-start = ((s32[8,16,512]{2,1,0:T(8,128)}), s32[8,16,512]{2,1,0:T(8,128)S(1)}, u32[]{:S(2)}, u32[]{:S(2)}) async-start(s32[8,16,512]{2,1,0:T(8,128)} %broadcast_in_dim.6), calls=%async_computation | async-start | bytes 524288 | tf_op jit(solution)/shard_map/all_to_all | solution.py:20
  11.1 8.2 %collective-permute-start.4 = (s32[16,512]{1,0:T(8,128)S(1)}, s32[16,512]{1,0:T(8,128)S(1)}, u32[]{:S(2)}, u32[]{:S(2)}) collective-permute-start(s32[16,512]{1,0:T(8,128)S(1)} %collective-permute-done.1), channel_id=1, source_target_pairs={{0,33},{1,32},{32,1},{33,0},{2,35},{3,34},{34,3},{35,2},{4,37},{5,... | collective-permute-start | bytes 98312 | tf_op jit(solution)/shard_map/ppermute | solution.py:43
  13.6 5.7 %collective-permute-start.3 = (s32[16,512]{1,0:T(8,128)S(1)}, s32[16,512]{1,0:T(8,128)S(1)}, u32[]{:S(2)}, u32[]{:S(2)}) collective-permute-start(s32[16,512]{1,0:T(8,128)S(1)} %collective-permute-done.1), channel_id=1, source_target_pairs={{0,1},{1,0},{2,3},{3,2},{4,5},{5,4},{6,7},{7,6},{8,9},{9,8},{10,11... | collective-permute-start | bytes 98312 | tf_op jit(solution)/shard_map/ppermute | solution.py:39
  13.8 5.4 %collective-permute-start.2 = (s32[16,512]{1,0:T(8,128)S(1)}, s32[16,512]{1,0:T(8,128)S(1)}, u32[]{:S(2)}, u32[]{:S(2)}) collective-permute-start(s32[16,512]{1,0:T(8,128)S(1)} %collective-permute-done.1), channel_id=1, source_target_pairs={{0,32},{32,0},{1,33},{33,1},{2,34},{34,2},{3,35},{35,3},{4,36},{36... | collective-permute-start | bytes 98312 | tf_op jit(solution)/shard_map/ppermute | solution.py:39
  19.3 9.2 %collective-permute-start.5 = (s32[64,512]{1,0:T(8,128)S(1)}, s32[64,512]{1,0:T(8,128)S(1)}, u32[]{:S(2)}, u32[]{:S(2)}) collective-permute-start(s32[64,512]{1,0:T(8,128)S(1)} %get-tuple-element.7), channel_id=1, source_target_pairs={{0,64},{64,128},{128,192},{192,0},{1,65},{65,129},{129,193},{193,1... | collective-permute-start | bytes 393224 | tf_op jit(solution)/shard_map/ppermute | solution.py:135
  22.0 6.4 %collective-permute-start.6 = (s32[64,512]{1,0:T(8,128)S(1)}, s32[64,512]{1,0:T(8,128)S(1)}, u32[]{:S(2)}, u32[]{:S(2)}) collective-permute-start(s32[64,512]{1,0:T(8,128)S(1)} %get-tuple-element.7), channel_id=1, source_target_pairs={{0,192},{64,0},{128,64},{192,128},{1,193},{65,1},{129,65},{193,129... | collective-permute-start | bytes 393224 | tf_op jit(solution)/shard_map/ppermute | solution.py:135
  24.9 6.6 %collective-permute-start.7 = (s32[64,512]{1,0:T(8,128)S(1)}, s32[64,512]{1,0:T(8,128)S(1)}, u32[]{:S(2)}, u32[]{:S(2)}) collective-permute-start(s32[64,512]{1,0:T(8,128)S(1)} %get-tuple-element.7), channel_id=1, source_target_pairs={{0,128},{64,192},{128,0},{192,64},{1,129},{65,193},{129,1},{193,65... | collective-permute-start | bytes 393224 | tf_op jit(solution)/shard_map/ppermute | solution.py:135
  28.5 3.0 %collective-permute-start.9 = (s32[8,512]{1,0:T(8,128)S(1)}, s32[8,512]{1,0:T(8,128)S(1)}, u32[]{:S(2)}, u32[]{:S(2)}) collective-permute-start(s32[8,512]{1,0:T(8,128)S(1)} %constant_dynamic-slice_fusion), channel_id=1, source_target_pairs={{0,16},{16,0},{1,17},{17,1},{2,18},{18,2},{3,19},{19,3},{4,20},{20... | collective-permute-start | bytes 49160 | tf_op jit(solution)/shard_map/ppermute | solution.py:39
  31.5 15.5 %collective-permute-start.8 = (s32[256,512]{1,0:T(8,128)S(1)}, s32[256,512]{1,0:T(8,128)S(1)}, u32[]{:S(2)}, u32[]{:S(2)}) collective-permute-start(s32[256,512]{1,0:T(8,128)S(1)} %constant_dynamic-update-slice_fusion.4.mine), channel_id=1, source_target_pairs={{0,16},{16,0},{1,17},{17,1},{2,18},{18,2},{3,19},{19,3},{4,20},{20... | collective-permute-start | bytes 1572872 | tf_op jit(solution)/shard_map/ppermute | solution.py:39
  32.3 14.6 %all-to-all-start.1 = ((s32[16,4,512]{2,1,0:T(4,128)}), s32[16,4,512]{2,1,0:T(4,128)S(1)}, u32[]{:S(2)}, u32[]{:S(2)}) async-start(s32[16,4,512]{2,1,0:T(4,128)} %bitcast.2), calls=%async_computation.1 | async-start | bytes 262144 | tf_op jit(solution)/shard_map/all_to_all | solution.py:152
  38.2 9.9 %collective-permute-start = (s32[128,512]{1,0:T(8,128)S(1)}, s32[128,512]{1,0:T(8,128)S(1)}, u32[]{:S(2)}, u32[]{:S(2)}) collective-permute-start(s32[128,512]{1,0:T(8,128)S(1)} %bitcast.10), channel_id=1, source_target_pairs={{0,1},{1,0},{2,3},{3,2},{4,5},{5,4},{6,7},{7,6},{8,9},{9,8},{10,11... | collective-permute-start | bytes 786440 | tf_op jit(solution)/shard_map/ppermute | solution.py:39

commit v2 on v1

--- a/solution.py
+++ b/solution.py
@@ -78,18 +78,24 @@
         jbuf[pl.ds(other, ROWS), :] = theirs[source, :]
 
 
-def counts_into(acc, base, i_ref, j_ref, thirds):
-    i_parts, j_parts, k_parts = pieces(i_ref[...]), pieces(j_ref[...]), pieces(thirds)
-    for i_part, j_part, k_part in zip(i_parts, j_parts, k_parts):
-        pairs = jnp.concatenate([i_part & k_part[t : t + 1] for t in range(4)], axis=0)
-        part = lax.dot_general(
-            jnp.concatenate([bits(pairs, b) for b in range(8)], axis=1),
-            jnp.concatenate([bits(j_part, b) for b in range(8)], axis=1),
-            (((1,), (1,)), ((), ())),
-            preferred_element_type=jnp.float32,
-        )
+def planes(words):
+    return jnp.concatenate([bits(words, b) for b in range(8)], axis=1)
+
+
+def product(i_part, j_planes, k_part):
+    pairs = jnp.concatenate([i_part & k_part[t : t + 1] for t in range(k_part.shape[0])], axis=0)
+    return lax.dot_general(
+        planes(pairs), j_planes, (((1,), (1,)), ((), ())), preferred_element_type=jnp.float32
+    )
+
+
+def counts_into(acc, base, i_ref, j_ref, thirds, keep=0):
+    parts = list(zip(pieces(i_ref[...]), pieces(j_ref[...]), pieces(thirds)))
+    for i_part, j_part, k_part in parts[: 4 - keep]:
+        part = product(i_part, planes(j_part), k_part)
         acc[...] = part if base is None else base[...] + part
         base = acc
+    return [(i_part, planes(j_part), k_part) for i_part, j_part, k_part in parts[4 - keep :]]
 
 
 def ones_of(i_ref, j_ref):
@@ -104,27 +110,38 @@
     return ones_i + ones_j
 
 
-def metric(iw, iw_x, mine, theirs, thirds, out, jbuf, jbuf_x, acc):
+def metric(section, iw, iw_x, mine, theirs, came, out, jbuf, jbuf_x, acc, rows, sems):
     place_j(mine, theirs, jbuf, 0)
     place_j(mine, theirs, jbuf_x, 1)
-    counts_into(acc, None, iw, jbuf, thirds[0:4])
-    counts_into(acc, acc, iw_x, jbuf_x, thirds[4:8])
-    ones_k = jnp.sum(popcounts(thirds[0:4]) + popcounts(thirds[4:8]), axis=1, keepdims=True)
+    half = lax.axis_index("xl")
+    root = ((section[0] * KS) // 256) * 2
+    k_own, k_other = came[root + half], came[root + 1 - half]
+    ones_k = jnp.sum(popcounts(k_own) + popcounts(k_other), axis=1, keepdims=True)
     ones_ij = ones_of(iw, jbuf) + ones_of(iw_x, jbuf_x) + 1.0
-    for t in range(4):
-        out[t] = 3.0 * acc[t * 128 : (t + 1) * 128, :] / (ones_ij + ones_k[t : t + 1])
+    counts_into(acc, None, iw, jbuf, k_own)
+    tail = counts_into(acc, acc, iw_x, jbuf_x, k_other, keep=1)
+    copies = [pltpu.make_async_copy(rows.at[t], out.at[t], sems.at[t]) for t in range(4)]
+    for i_part, j_planes, k_part in tail:
+        for pair in range(0, 4, 2):
+            part = product(i_part, j_planes, k_part[pair : pair + 2])
+            for t in (pair, pair + 1):
+                counts = acc[t * 128 : (t + 1) * 128, :] + part[(t - pair) * 128 : (t - pair + 1) * 128]
+                rows[t] = 3.0 * counts / (ones_ij + ones_k[t : t + 1])
+                copies[t].start()
+    for copy in copies:
+        copy.wait()
 
 
-def on_core(kernel, operands, outs, scratch):
+def on_core(kernel, operands, section, outs, scratch):
     operands = [pltpu.with_memory_space_constraint(a, pltpu.VMEM) for a in operands]
     return pl.pallas_call(
         kernel,
         out_shape=outs,
-        in_specs=[VM] * len(operands),
-        out_specs=jax.tree.map(lambda _: VM, outs),
-        scratch_shapes=[pltpu.VMEM(*s) for s in scratch],
+        in_specs=[pl.BlockSpec(memory_space=pltpu.SMEM)] + [VM] * len(operands),
+        out_specs=pl.BlockSpec(memory_space=pl.ANY),
+        scratch_shapes=scratch,
         cost_estimate=COST,
-    )(*operands)
+    )(section, *operands)
 
 
 VM = pl.BlockSpec(memory_space=pltpu.VMEM)
@@ -137,7 +154,6 @@
 
 def per_device(alleles, section):
     words = alleles.shape[1]
-    half = lax.axis_index("xl")
     row = section[0] * KS
     ia_s = row // 128
     moved = to_planes(alleles)
@@ -149,21 +165,24 @@
     slab = lax.dynamic_slice_in_dim(iwords, lax.rem(row, 128), KS, 0)
     slab = spread(slab, "c", 1, lax.rem(ia_s, 2))
     slab = jnp.broadcast_to(slab.reshape(1, 2, 4, words), (8, 2, 4, words)).reshape(16, 4, words)
-    came = lax.all_to_all(slab, (*SIDE, "xl"), 0, 0, tiled=True).reshape(8, 2, 4, words)
-    came = lax.dynamic_index_in_dim(came, ia_s // 2, 0, keepdims=False)
-    k_own = lax.dynamic_index_in_dim(came, half, 0, keepdims=False)
-    k_other = lax.dynamic_index_in_dim(came, 1 - half, 0, keepdims=False)
-    thirds = jnp.concatenate([k_own, k_other], axis=0)
+    came = lax.all_to_all(slab, (*SIDE, "xl"), 0, 0, tiled=True)
     iwords_x = swap(iwords, "xl")
     turns = [turn(quad, d) for d in Y_STEPS[1:]]
     mine = jnp.concatenate([quad, *turns], axis=0)
     theirs = swap(mine, "c")
-    j_words = ((256, words), jnp.int32)
+    j_words = pltpu.VMEM((256, words), jnp.int32)
     return on_core(
         metric,
-        [iwords, iwords_x, mine, theirs, thirds],
+        [iwords, iwords_x, mine, theirs, came],
+        section,
         jax.ShapeDtypeStruct((4, 128, 256), jnp.float32),
-        [j_words, j_words, ((512, 256), jnp.float32)],
+        [
+            j_words,
+            j_words,
+            pltpu.VMEM((512, 256), jnp.float32),
+            pltpu.VMEM((4, 128, 256), jnp.float32),
+            pltpu.SemaphoreType.DMA((4,)),
+        ],
     )
 
 

time: 54.3 us -> 58.4 us (1.076)
  the two profiles are of different devices: /device:TPU:32 before, /device:TPU:1 now
where the time goes in v2:
time: 58.4 us; the launch traced here: 58.1 us
  starting transfers between devices  32.2 us (55%)
  blocking collectives  9.43 us (16%)
  waiting for transfers between devices  8.69 us (15%)
  Pallas kernels  5.5 us (9%)
  local copies, waits for them, and re-layouts  1.47 us (3%)
  between operations  0.76 us (1%)
    ppermute x5, starting transfers between devices, swap(): lax.ppermute(array, axis, [(n, n ^ bit) for n in range(lax.axis_size(axis...  11.6 us
    all_to_all x1, blocking collectives, per_device(): came = lax.all_to_all(slab, (*SIDE, 'xl'), 0, 0, tiled=True)  9.43 us
    all_to_all x1, starting transfers between devices, broadcast_all(): lax.all_to_all(jnp.broadcast_to(array[None], (size, *array.shape)), axis,...  8.2 us
    ppermute x1, starting transfers between devices, to_planes(): return lax.ppermute(array, ('y', 'xh', 'c', 'z'), pairs)  6.19 us
    pallas_call x1, Pallas kernels, on_core(): pl.pallas_call(kernel, out_shape=outs, in_specs=[pl.BlockSpec(memory_spac...  5.5 us
    ppermute x3, starting transfers between devices, turn(): return lax.ppermute(array, 'y', [(n, (n + step) % 4) for n in range(4)])  3.72 us
    ppermute x1, waiting for transfers between devices, to_planes(): return lax.ppermute(array, ('y', 'xh', 'c', 'z'), pairs)  3.09 us
    ppermute x5, waiting for transfers between devices, swap(): lax.ppermute(array, axis, [(n, n ^ bit) for n in range(lax.axis_size(axis...  2.9 us
  transfers between devices with their start and end apart: 11, of which 4 were waited for; matrix products, arithmetic and copies ran while one was open for 1% of the time, Pallas kernels for 0%

profile of v2, /device:TPU:1, one launch (start us, length us, event | category | flops | bytes accessed | tf_op | source)
XLA Modules:
  0.0 58.1 jit_solution(11944763648463570470)
XLA Ops:
  0.0 6.2 %collective-permute-start.1 = (s32[16,512]{1,0:T(8,128)}, s32[16,512]{1,0:T(8,128)S(1)}, u32[]{:S(2)}, u32[]{:S(2)}) collective-permute-start(s32[16,512]{1,0:T(8,128)} %param.2), channel_id=1, source_target_pairs={{0,160},{2,96},{4,128},{6,64},{8,0},{10,192},{12,32},{14,224},{16,... | collective-permute-start | bytes 98312 | tf_op jit(solution)/shard_map/ppermute | solution.py:35
  6.2 3.1 %collective-permute-done.1 = s32[16,512]{1,0:T(8,128)S(1)} collective-permute-done((s32[16,512]{1,0:T(8,128)}, s32[16,512]{1,0:T(8,128)S(1)}, u32[]{:S(2)}, u32[]{:S(2)}) %collective-permute-start.1) | collective-permute-done | bytes 32800 | tf_op jit(solution)/shard_map/ppermute | solution.py:35
  9.3 2.5 %collective-permute-start.4 = (s32[16,512]{1,0:T(8,128)S(1)}, s32[16,512]{1,0:T(8,128)S(1)}, u32[]{:S(2)}, u32[]{:S(2)}) collective-permute-start(s32[16,512]{1,0:T(8,128)S(1)} %collective-permute-done.1), channel_id=1, source_target_pairs={{0,33},{1,32},{32,1},{33,0},{2,35},{3,34},{34,3},{35,2},{4,37},{5,... | collective-permute-start | bytes 98312 | tf_op jit(solution)/shard_map/ppermute | solution.py:43
  11.8 0.0 collective-permute-start.3
  11.8 1.4 %collective-permute-start.2 = (s32[16,512]{1,0:T(8,128)S(1)}, s32[16,512]{1,0:T(8,128)S(1)}, u32[]{:S(2)}, u32[]{:S(2)}) collective-permute-start(s32[16,512]{1,0:T(8,128)S(1)} %collective-permute-done.1), channel_id=1, source_target_pairs={{0,32},{32,0},{1,33},{33,1},{2,34},{34,2},{3,35},{35,3},{4,36},{36... | collective-permute-start | bytes 98312 | tf_op jit(solution)/shard_map/ppermute | solution.py:39
  13.2 2.9 %collective-permute-done.2 = s32[16,512]{1,0:T(8,128)S(1)} collective-permute-done((s32[16,512]{1,0:T(8,128)S(1)}, s32[16,512]{1,0:T(8,128)S(1)}, u32[]{:S(2)}, u32[]{:S(2)}) %collective-permute-start.2) | collective-permute-done | bytes 32800 | tf_op jit(solution)/shard_map/ppermute | solution.py:39
  16.0 0.0 collective-permute-done.3
  16.1 0.0 collective-permute-done.4
  16.1 0.0 copy-start
  16.1 0.1 collective-permute-start.5
  16.2 0.6 %copy-done = s32[16,512]{1,0:T(8,128)S(1)} copy-done((s32[16,512]{1,0:T(8,128)S(1)}, s32[16,512]{1,0:T(8,128)}, u32[]{:S(2)}) %copy-start) | copy-done | bytes 32792
  16.8 0.7 %broadcast_in_dim.6 = s32[8,16,512]{2,1,0:T(8,128)} broadcast(s32[16,512]{1,0:T(8,128)S(1)} %copy-done), dimensions={1,2} | broadcast | bytes 294912 | tf_op jit(solution)/shard_map/broadcast_in_dim | solution.py:21
  17.6 8.2 %all-to-all-start = ((s32[8,16,512]{2,1,0:T(8,128)}), s32[8,16,512]{2,1,0:T(8,128)S(1)}, u32[]{:S(2)}, u32[]{:S(2)}) async-start(s32[8,16,512]{2,1,0:T(8,128)} %broadcast_in_dim.6), calls=%async_computation | async-start | bytes 524288 | tf_op jit(solution)/shard_map/all_to_all | solution.py:20
  25.8 1.0 %collective-permute-start.6 = (s32[64,512]{1,0:T(8,128)S(1)}, s32[64,512]{1,0:T(8,128)S(1)}, u32[]{:S(2)}, u32[]{:S(2)}) collective-permute-start(s32[64,512]{1,0:T(8,128)S(1)} %get-tuple-element.5), channel_id=1, source_target_pairs={{0,192},{64,0},{128,64},{192,128},{1,193},{65,1},{129,65},{193,129... | collective-permute-start | bytes 393224 | tf_op jit(solution)/shard_map/ppermute | solution.py:152
  26.8 2.6 %collective-permute-start.7 = (s32[64,512]{1,0:T(8,128)S(1)}, s32[64,512]{1,0:T(8,128)S(1)}, u32[]{:S(2)}, u32[]{:S(2)}) collective-permute-start(s32[64,512]{1,0:T(8,128)S(1)} %get-tuple-element.5), channel_id=1, source_target_pairs={{0,128},{64,192},{128,0},{192,64},{1,129},{65,193},{129,1},{193,65... | collective-permute-start | bytes 393224 | tf_op jit(solution)/shard_map/ppermute | solution.py:152
  29.4 0.0 collective-permute-done.5
  29.4 0.5 collective-permute-done.6
  30.0 2.1 %collective-permute-done.7 = s32[64,512]{1,0:T(8,128)S(1)} collective-permute-done((s32[64,512]{1,0:T(8,128)S(1)}, s32[64,512]{1,0:T(8,128)S(1)}, u32[]{:S(2)}, u32[]{:S(2)}) %collective-permute-start.7) | collective-permute-done | bytes 131104 | tf_op jit(solution)/shard_map/ppermute | solution.py:152
  32.1 5.4 %collective-permute-start.8 = (s32[256,512]{1,0:T(8,128)S(1)}, s32[256,512]{1,0:T(8,128)S(1)}, u32[]{:S(2)}, u32[]{:S(2)}) collective-permute-start(s32[256,512]{1,0:T(8,128)S(1)} %constant_dynamic-update-slice_fusion.4.mine), channel_id=1, source_target_pairs={{0,16},{16,0},{1,17},{17,1},{2,18},{18,2},{3,19},{19,3},{4,20},{20... | collective-permute-start | bytes 1572872 | tf_op jit(solution)/shard_map/ppermute | solution.py:39
  38.2 0.0 all-to-all-done
  38.2 3.1 %collective-permute-start.9 = (s32[8,512]{1,0:T(8,128)S(1)}, s32[8,512]{1,0:T(8,128)S(1)}, u32[]{:S(2)}, u32[]{:S(2)}) collective-permute-start(s32[8,512]{1,0:T(8,128)S(1)} %constant_dynamic-slice_fusion), channel_id=1, source_target_pairs={{0,16},{16,0},{1,17},{17,1},{2,18},{18,2},{3,19},{19,3},{4,20},{20... | collective-permute-start | bytes 49160 | tf_op jit(solution)/shard_map/ppermute | solution.py:39
  41.4 1.7 %collective-permute-start = (s32[128,512]{1,0:T(8,128)S(1)}, s32[128,512]{1,0:T(8,128)S(1)}, u32[]{:S(2)}, u32[]{:S(2)}) collective-permute-start(s32[128,512]{1,0:T(8,128)S(1)} %bitcast.4), channel_id=1, source_target_pairs={{0,1},{1,0},{2,3},{3,2},{4,5},{5,4},{6,7},{7,6},{8,9},{9,8},{10,11... | collective-permute-start | bytes 786440 | tf_op jit(solution)/shard_map/ppermute | solution.py:39
  43.1 0.0 collective-permute-done.9
  43.1 9.4 %all_to_all.10.came = s32[16,4,512]{2,1,0:T(4,128)S(1)} all-to-all(s32[16,4,512]{2,1,0:T(4,128)S(1)} %bitcast.7), channel_id=1, replica_groups=mesh['y'=4,'xh'=2,'c'=2,'z'=8,'xl'=2] {'y','xh','xl'}, dimensions={0} | all-to-all | bytes 262144 | tf_op jit(solution)/shard_map/all_to_all | solution.py:168
  52.6 0.0 collective-permute-done.8.theirs
  52.6 0.0 collective-permute-done.iw_x
  52.6 5.5 %shard_map.28 = f32[4,128,256]{2,1,0:T(8,128)} custom-call(s32[1]{0:T(128)S(6)} %copy.12.section, s32[128,512]{1,0:T(8,128)S(1)} %bitcast.6, s32[128,512]{1,0:T(8,128)S(1)} %collective-permute-done.iw_x, s32[256,512]{1,0:T(8,128)S(1)} %constant_dynamic-update-slice_fusion.4.mine, s32[256,512]{1,0:T(8,128)S(1)} %collective-permute-done.8.theirs, ...), custom_call_target="tpu_custom_call" | custom-call | flops 8589934592 | bytes 2097152 | tf_op jit(solution)/shard_map/pallas_call | solution.py:137
  (11 shorter events, 0.1 us)
Async XLA Ops:
  0.0 9.3 %collective-permute-start.1 = (s32[16,512]{1,0:T(8,128)}, s32[16,512]{1,0:T(8,128)S(1)}, u32[]{:S(2)}, u32[]{:S(2)}) collective-permute-start(s32[16,512]{1,0:T(8,128)} %param.2), channel_id=1, source_target_pairs={{0,160},{2,96},{4,128},{6,64},{8,0},{10,192},{12,32},{14,224},{16,... | collective-permute-start | bytes 98312 | tf_op jit(solution)/shard_map/ppermute | solution.py:35
  9.3 6.8 %collective-permute-start.4 = (s32[16,512]{1,0:T(8,128)S(1)}, s32[16,512]{1,0:T(8,128)S(1)}, u32[]{:S(2)}, u32[]{:S(2)}) collective-permute-start(s32[16,512]{1,0:T(8,128)S(1)} %collective-permute-done.1), channel_id=1, source_target_pairs={{0,33},{1,32},{32,1},{33,0},{2,35},{3,34},{34,3},{35,2},{4,37},{5,... | collective-permute-start | bytes 98312 | tf_op jit(solution)/shard_map/ppermute | solution.py:43
  11.8 4.3 %collective-permute-start.3 = (s32[16,512]{1,0:T(8,128)S(1)}, s32[16,512]{1,0:T(8,128)S(1)}, u32[]{:S(2)}, u32[]{:S(2)}) collective-permute-start(s32[16,512]{1,0:T(8,128)S(1)} %collective-permute-done.1), channel_id=1, source_target_pairs={{0,1},{1,0},{2,3},{3,2},{4,5},{5,4},{6,7},{7,6},{8,9},{9,8},{10,11... | collective-permute-start | bytes 98312 | tf_op jit(solution)/shard_map/ppermute | solution.py:39
  11.8 4.3 %collective-permute-start.2 = (s32[16,512]{1,0:T(8,128)S(1)}, s32[16,512]{1,0:T(8,128)S(1)}, u32[]{:S(2)}, u32[]{:S(2)}) collective-permute-start(s32[16,512]{1,0:T(8,128)S(1)} %collective-permute-done.1), channel_id=1, source_target_pairs={{0,32},{32,0},{1,33},{33,1},{2,34},{34,2},{3,35},{35,3},{4,36},{36... | collective-permute-start | bytes 98312 | tf_op jit(solution)/shard_map/ppermute | solution.py:39
  16.1 0.8 %copy-start = (s32[16,512]{1,0:T(8,128)S(1)}, s32[16,512]{1,0:T(8,128)}, u32[]{:S(2)}) copy-start(s32[16,512]{1,0:T(8,128)} %param.2) | copy-start | bytes 98308
  16.1 13.3 %collective-permute-start.5 = (s32[64,512]{1,0:T(8,128)S(1)}, s32[64,512]{1,0:T(8,128)S(1)}, u32[]{:S(2)}, u32[]{:S(2)}) collective-permute-start(s32[64,512]{1,0:T(8,128)S(1)} %get-tuple-element.5), channel_id=1, source_target_pairs={{0,64},{64,128},{128,192},{192,0},{1,65},{65,129},{129,193},{193,1... | collective-permute-start | bytes 393224 | tf_op jit(solution)/shard_map/ppermute | solution.py:152
  17.6 20.6 %all-to-all-start = ((s32[8,16,512]{2,1,0:T(8,128)}), s32[8,16,512]{2,1,0:T(8,128)S(1)}, u32[]{:S(2)}, u32[]{:S(2)}) async-start(s32[8,16,512]{2,1,0:T(8,128)} %broadcast_in_dim.6), calls=%async_computation | async-start | bytes 524288 | tf_op jit(solution)/shard_map/all_to_all | solution.py:20
  25.8 4.2 %collective-permute-start.6 = (s32[64,512]{1,0:T(8,128)S(1)}, s32[64,512]{1,0:T(8,128)S(1)}, u32[]{:S(2)}, u32[]{:S(2)}) collective-permute-start(s32[64,512]{1,0:T(8,128)S(1)} %get-tuple-element.5), channel_id=1, source_target_pairs={{0,192},{64,0},{128,64},{192,128},{1,193},{65,1},{129,65},{193,129... | collective-permute-start | bytes 393224 | tf_op jit(solution)/shard_map/ppermute | solution.py:152
  26.8 5.3 %collective-permute-start.7 = (s32[64,512]{1,0:T(8,128)S(1)}, s32[64,512]{1,0:T(8,128)S(1)}, u32[]{:S(2)}, u32[]{:S(2)}) collective-permute-start(s32[64,512]{1,0:T(8,128)S(1)} %get-tuple-element.5), channel_id=1, source_target_pairs={{0,128},{64,192},{128,0},{192,64},{1,129},{65,193},{129,1},{193,65... | collective-permute-start | bytes 393224 | tf_op jit(solution)/shard_map/ppermute | solution.py:152
  32.1 20.4 %collective-permute-start.8 = (s32[256,512]{1,0:T(8,128)S(1)}, s32[256,512]{1,0:T(8,128)S(1)}, u32[]{:S(2)}, u32[]{:S(2)}) collective-permute-start(s32[256,512]{1,0:T(8,128)S(1)} %constant_dynamic-update-slice_fusion.4.mine), channel_id=1, source_target_pairs={{0,16},{16,0},{1,17},{17,1},{2,18},{18,2},{3,19},{19,3},{4,20},{20... | collective-permute-start | bytes 1572872 | tf_op jit(solution)/shard_map/ppermute | solution.py:39
  38.2 4.9 %collective-permute-start.9 = (s32[8,512]{1,0:T(8,128)S(1)}, s32[8,512]{1,0:T(8,128)S(1)}, u32[]{:S(2)}, u32[]{:S(2)}) collective-permute-start(s32[8,512]{1,0:T(8,128)S(1)} %constant_dynamic-slice_fusion), channel_id=1, source_target_pairs={{0,16},{16,0},{1,17},{17,1},{2,18},{18,2},{3,19},{19,3},{4,20},{20... | collective-permute-start | bytes 49160 | tf_op jit(solution)/shard_map/ppermute | solution.py:39
  41.4 11.2 %collective-permute-start = (s32[128,512]{1,0:T(8,128)S(1)}, s32[128,512]{1,0:T(8,128)S(1)}, u32[]{:S(2)}, u32[]{:S(2)}) collective-permute-start(s32[128,512]{1,0:T(8,128)S(1)} %bitcast.4), channel_id=1, source_target_pairs={{0,1},{1,0},{2,3},{3,2},{4,5},{5,4},{6,7},{7,6},{8,9},{9,8},{10,11... | collective-permute-start | bytes 786440 | tf_op jit(solution)/shard_map/ppermute | solution.py:39
